TPU v7x, 32 devices: a whole 2x2x4 slice. The times are simulated.
32 devices in a mesh: gx: 8 (over y, x, core), gy: 4 (over z).
Axes of the slice: x: 2, y: 2, z: 4, core: 2. Of those that a mesh axis runs over, the one named last changes fastest.
Arguments:
- probes: float32 [16, 128, 128, 256], P(None, 'gx', 'gy'), may hold values from -6 to 6
- diffusivity: float32 [128, 128, 256], P('gx', 'gy'), may hold values from 0.5 to 2
- wind_speed: float32 [3], replicated, may hold values from 0.5 to 2
- sensor_cell: int32 [8, 4, 128], P('gx', 'gy'), may hold values from 0 to 131071
- sensor_owner: int32 [8, 4, 128, 1], P('gx', 'gy'), may hold values from 0 to 31; in each aligned block of 128 rows (0 to 127, 128 to 255, ..., all dimensions but the last counted through in order) at most 4 rows name the same one
- sensor_count: int32 [8, 4], P('gx', 'gy'), may hold values from 64 to 128
- goal_weight: float32 [8, 4, 128, 16], P('gx', 'gy'), may hold values from -0.6 to 0.6
Outputs:
- fields: float32 [16, 128, 128, 256], P(None, 'gx', 'gy')
- goal_block: float32 [512, 16], P(('gx', 'gy'))
- ritz_gram: float32 [16, 16], replicated
Inputs may be any that keep to these rules, and one draw needn't show every extreme that they name: `sensor_owner`: among the rows of one device, no owner is named more than 4 times, a bound that some block reaches.
All inputs are finite; a program needn't handle non-finite values.
Results may differ from a plain program's by a relative error of at most 0.0003.
Values sent between devices are 32-bit elements; how exact they have to be, the bound alone decides.
A program may use at most 192 MiB of HBM per device.

v0:
```python
import jax
import jax.numpy as jnp
from jax import lax
from jax.sharding import PartitionSpec as P

STEPS = 2
SWEEPS = 4
time_step = 2.0


def padded_2(cells, sides, width):
    for axis, dim in sides:
        count = lax.axis_size(axis)
        ends = count - 1
        head = lax.slice_in_dim(cells, 0, width, axis=dim)
        tail = lax.slice_in_dim(cells, cells.shape[dim] - width, cells.shape[dim], axis=dim)
        cells = jnp.concatenate(
            [
                lax.ppermute(tail, axis, [(i, (i + 1) % count) for i in range(ends)]),
                cells,
                lax.ppermute(head, axis, [((i + 1) % count, i) for i in range(ends)]),
            ],
            axis=dim,
        )
    return cells


def relax(padded, source, diffusion, wind_speed):
    centre = padded[..., 1:-1, 1:-1, :]
    widths = [(0, 0)] * (centre.ndim - 1) + [(1, 1)]
    zpadded = jnp.pad(centre, widths)
    beside = padded[..., 2:, 1:-1, :] + padded[..., :-2, 1:-1, :]
    beside = beside + padded[..., 1:-1, 2:, :] + padded[..., 1:-1, :-2, :]
    beside = beside + zpadded[..., 2:] + zpadded[..., :-2]
    upwind = (
        wind_speed[0] * padded[..., :-2, 1:-1, :]
        + wind_speed[1] * padded[..., 1:-1, :-2, :]
        + wind_speed[2] * zpadded[..., :-2]
    )
    diagonal = 1.0 + time_step * (6.0 * diffusion + wind_speed[0] + wind_speed[1] + wind_speed[2])
    updated = (source + time_step * (diffusion * beside + upwind)) / diagonal
    return jnp.where(diffusion > 0.0, updated, 0.0)


def body(probes, diffusivity, wind_speed, sensor_cell, sensor_owner, sensor_count, goal_weight):
    state_field = probes
    for step_index in range(STEPS):
        source = state_field
        for sweep_index in range(SWEEPS):
            padded = padded_2(state_field, (("gx", 1), ("gy", 2)), 1)
            state_field = relax(padded, source, diffusivity, wind_speed)
    probe_count = state_field.shape[0]
    sensor_rows = sensor_cell.shape[2]
    goal_count = goal_weight.shape[3]
    device_count = lax.axis_size("gx") * lax.axis_size("gy")
    capacity = max(2, (sensor_rows + device_count - 1) // device_count)
    flattened = state_field.reshape(probe_count, -1)
    readings = jnp.take(flattened, sensor_cell.reshape(-1), axis=1)
    row_index = jnp.arange(sensor_rows, dtype=jnp.int32)
    active = (row_index < sensor_count.reshape(())).astype(jnp.float32)
    readings = readings.T * active[:, None]
    weights = goal_weight.reshape(sensor_rows, goal_count)
    owners = sensor_owner.reshape(sensor_rows)
    earlier = (owners[None, :] == owners[:, None]) & (row_index[None, :] < row_index[:, None])
    slot_rank = jnp.sum(earlier.astype(jnp.int32), axis=1)
    slot_index = owners * capacity + slot_rank
    placing = (
        jnp.arange(device_count * capacity, dtype=jnp.int32)[:, None] == slot_index[None, :]
    ).astype(jnp.float32)
    payload = jnp.concatenate([readings, weights], axis=1)
    outgoing = jnp.dot(placing, payload, precision=lax.Precision.HIGHEST).reshape(
        device_count, capacity, probe_count + goal_count
    )
    received = lax.all_to_all(outgoing, ("gx", "gy"), split_axis=0, concat_axis=0, tiled=True)
    goal_block = jnp.einsum(
        "scj,scp->jp",
        received[..., probe_count:],
        received[..., :probe_count],
        precision=lax.Precision.HIGHEST,
    )
    ritz_gram = lax.psum(
        jnp.dot(goal_block.T, goal_block, precision=lax.Precision.HIGHEST), ("gx", "gy")
    )
    return (state_field, goal_block, ritz_gram)


def solution(mesh):
    placed = (
        P(None, "gx", "gy", None),
        P("gx", "gy", None),
        P(),
        P("gx", "gy", None),
        P("gx", "gy", None, None),
        P("gx", "gy"),
        P("gx", "gy", None, None),
    )
    return jax.shard_map(
        body,
        mesh=mesh,
        in_specs=placed,
        out_specs=(P(None, "gx", "gy", None), P(("gx", "gy"), None), P()),
        check_vma=False,
    )
```

profile of v0, /device:TPU:0, one launch (start us, length us, event | category | flops | bytes accessed | tf_op | source)
XLA Modules:
  0.0 530.0 jit_solution(1779432885856855623)
XLA Ops:
  0.7 10.1 %copy.60 = f32[16,16,32,256]{3,0,2,1:T(8,128)S(1)} copy(f32[16,16,32,256]{3,2,1,0:T(8,128)} %param.7) | data formatting | bytes 16777216 | tf_op args[0]
  16.0 10.0 %constant_dynamic-update-slice_fusion.1 = f32[16,18,32,256]{3,0,2,1:T(8,128)} fusion(f32[16,18,32,256]{3,0,2,1:T(8,128)} %constant_dynamic-update-slice_fusion.2, f32[16,16,32,256]{3,2,1,0:T(8,128)S(1)} %copy-done), kind=kLoop, calls=%fused_computation.202 | loop fusion | bytes 16777216
  29.3 4.9 collective-permute-start.3
  38.4 25.3 %fusion.81 = f32[16,16,32,256]{3,0,2,1:T(8,128)} fusion(f32[16,16,32,256]{3,0,2,1:T(8,128)} %copy-done.2, f32[16,18,32,256]{3,0,2,1:T(8,128)} %constant_dynamic-update-slice_fusion, f32[16,18,1,256]{3,0,2,1:T(8,128)S(1)} %collective-permute-done.3, f32[16,18,1,256]{3,0,2,1:T(8,128)S(1)} %collective-permute-done.2, ...), kind=kLoop, calls=%fused_computation.158 | loop fusion | flops 41943040 | bytes 29032460 | tf_op jit(solution)/shard_map/jit(_where)/select_n | solution.py:42
  66.3 7.8 %collective-permute-start.5 = (f32[16,1,32,256]{3,0,2,1:T(8,128)S(1)}, f32[16,1,32,256]{3,0,2,1:T(8,128)S(1)}, u32[]{:S(2)}, u32[]{:S(2)}) collective-permute-start(f32[16,1,32,256]{3,0,2,1:T(8,128)S(1)} %get-tuple-element.40), channel_id=1, source_target_pairs={{0,4},{4,8},{8,12},{12,16},{16,20},{20,24},{24,28},{1,5},{5,9},{9,... | collective-permute-start | bytes 1572872 | tf_op jit(solution)/shard_map/ppermute | solution.py:19
  78.0 4.9 collective-permute-start.7
  86.9 24.8 %fusion.87 = f32[16,16,32,256]{3,0,2,1:T(8,128)} fusion(f32[16,16,32,256]{3,0,2,1:T(8,128)} %fusion.81, f32[16,1,32,256]{3,0,2,1:T(8,128)S(1)} %collective-permute-done.4, f32[16,1,32,256]{3,0,2,1:T(8,128)S(1)} %collective-permute-done.5, f32[16,18,1,256]{3,0,2,1:T(8,128)S(1)} %collective-permute-done.7, f32[16,18,1,256]{3,0,2,1:T(8,128)S(1)} %collective-permute-done.6, ...), kind=kLoop, calls=%fused_computation.164 | loop fusion | flops 50331648 | bytes 27983884 | tf_op jit(solution)/shard_map/jit(_where)/select_n | solution.py:42
  114.4 12.9 %collective-permute-start.9 = (f32[16,1,32,256]{3,0,2,1:T(8,128)S(1)}, f32[16,1,32,256]{3,0,2,1:T(8,128)S(1)}, u32[]{:S(2)}, u32[]{:S(2)}) collective-permute-start(f32[16,1,32,256]{3,0,2,1:T(8,128)S(1)} %get-tuple-element.38), channel_id=1, source_target_pairs={{0,4},{4,8},{8,12},{12,16},{16,20},{20,24},{24,28},{1,5},{5,9},{9,... | collective-permute-start | bytes 1572872 | tf_op jit(solution)/shard_map/ppermute | solution.py:19
  140.1 24.8 %fusion.86 = f32[16,16,32,256]{3,0,2,1:T(8,128)} fusion(f32[16,16,32,256]{3,0,2,1:T(8,128)} %fusion.87, f32[16,1,32,256]{3,0,2,1:T(8,128)S(1)} %collective-permute-done.8, f32[16,1,32,256]{3,0,2,1:T(8,128)S(1)} %collective-permute-done.9, f32[16,18,1,256]{3,0,2,1:T(8,128)S(1)} %collective-permute-done.11, ...), kind=kLoop, calls=%fused_computation.163 | loop fusion | flops 50331648 | bytes 27983884 | tf_op jit(solution)/shard_map/jit(_where)/select_n | solution.py:42
  167.4 10.1 %collective-permute-start.13 = (f32[16,1,32,256]{3,0,2,1:T(8,128)S(1)}, f32[16,1,32,256]{3,0,2,1:T(8,128)S(1)}, u32[]{:S(2)}, u32[]{:S(2)}) collective-permute-start(f32[16,1,32,256]{3,0,2,1:T(8,128)S(1)} %get-tuple-element.36), channel_id=1, source_target_pairs={{0,4},{4,8},{8,12},{12,16},{16,20},{20,24},{24,28},{1,5},{5,9},{9,... | collective-permute-start | bytes 1572872 | tf_op jit(solution)/shard_map/ppermute | solution.py:19
  190.5 24.2 %fusion.85 = f32[16,16,32,256]{3,0,2,1:T(8,128)S(1)} fusion(f32[16,16,32,256]{3,0,2,1:T(8,128)} %fusion.86, f32[16,1,32,256]{3,0,2,1:T(8,128)S(1)} %collective-permute-done.12, f32[16,1,32,256]{3,0,2,1:T(8,128)S(1)} %collective-permute-done.13, f32[16,18,1,256]{3,0,2,1:T(8,128)S(1)} %collective-permute-done.15, ...), kind=kLoop, calls=%fused_computation.162 | loop fusion | flops 50331648 | bytes 27983884 | tf_op jit(solution)/shard_map/jit(_where)/select_n | solution.py:42
  216.1 9.8 %collective-permute-start.17 = (f32[16,1,32,256]{3,0,2,1:T(8,128)S(1)}, f32[16,1,32,256]{3,0,2,1:T(8,128)S(1)}, u32[]{:S(2)}, u32[]{:S(2)}) collective-permute-start(f32[16,1,32,256]{3,0,2,1:T(8,128)S(1)} %get-tuple-element.34), channel_id=1, source_target_pairs={{0,4},{4,8},{8,12},{12,16},{16,20},{20,24},{24,28},{1,5},{5,9},{9,... | collective-permute-start | bytes 1572872 | tf_op jit(solution)/shard_map/ppermute | solution.py:19
  228.7 5.1 collective-permute-start.19
  237.8 13.1 %fusion.80 = f32[16,16,32,256]{3,0,2,1:T(8,128)} fusion(f32[16,16,32,256]{3,0,2,1:T(8,128)S(1)} %fusion.85, f32[16,1,32,256]{3,0,2,1:T(8,128)S(1)} %collective-permute-done.16, f32[16,1,32,256]{3,0,2,1:T(8,128)S(1)} %collective-permute-done.17, f32[16,18,1,256]{3,0,2,1:T(8,128)S(1)} %collective-permute-done.19, ...), kind=kLoop, calls=%fused_computation.157 | loop fusion | flops 50331648 | bytes 19595276 | tf_op jit(solution)/shard_map/jit(_where)/select_n | solution.py:42
  253.5 9.8 %collective-permute-start.21 = (f32[16,1,32,256]{3,0,2,1:T(8,128)S(1)}, f32[16,1,32,256]{3,0,2,1:T(8,128)S(1)}, u32[]{:S(2)}, u32[]{:S(2)}) collective-permute-start(f32[16,1,32,256]{3,0,2,1:T(8,128)S(1)} %get-tuple-element.32), channel_id=1, source_target_pairs={{0,4},{4,8},{8,12},{12,16},{16,20},{20,24},{24,28},{1,5},{5,9},{9,... | collective-permute-start | bytes 1572872 | tf_op jit(solution)/shard_map/ppermute | solution.py:19
  276.2 22.7 %fusion.84 = f32[16,16,32,256]{3,0,2,1:T(8,128)} fusion(f32[16,16,32,256]{3,0,2,1:T(8,128)S(1)} %fusion.85, f32[16,16,32,256]{3,0,2,1:T(8,128)} %fusion.80, f32[16,1,32,256]{3,0,2,1:T(8,128)S(1)} %collective-permute-done.20, f32[16,1,32,256]{3,0,2,1:T(8,128)S(1)} %collective-permute-done.21, f32[16,18,1,256]{3,0,2,1:T(8,128)S(1)} %collective-permute-done.23, ...), kind=kLoop, calls=%fused_computation.161 | loop fusion | flops 50331648 | bytes 27983884 | tf_op jit(solution)/shard_map/jit(_where)/select_n | solution.py:42
  301.5 11.3 %collective-permute-start.25 = (f32[16,1,32,256]{3,0,2,1:T(8,128)S(1)}, f32[16,1,32,256]{3,0,2,1:T(8,128)S(1)}, u32[]{:S(2)}, u32[]{:S(2)}) collective-permute-start(f32[16,1,32,256]{3,0,2,1:T(8,128)S(1)} %get-tuple-element.30), channel_id=1, source_target_pairs={{0,4},{4,8},{8,12},{12,16},{16,20},{20,24},{24,28},{1,5},{5,9},{9,... | collective-permute-start | bytes 1572872 | tf_op jit(solution)/shard_map/ppermute | solution.py:19
  325.6 22.7 %fusion.83 = f32[16,16,32,256]{3,0,2,1:T(8,128)} fusion(f32[16,16,32,256]{3,0,2,1:T(8,128)S(1)} %fusion.85, f32[16,16,32,256]{3,0,2,1:T(8,128)} %fusion.84, f32[16,1,32,256]{3,0,2,1:T(8,128)S(1)} %collective-permute-done.24, f32[16,1,32,256]{3,0,2,1:T(8,128)S(1)} %collective-permute-done.25, f32[16,18,1,256]{3,0,2,1:T(8,128)S(1)} %collective-permute-done.27, ...), kind=kLoop, calls=%fused_computation.160 | loop fusion | flops 50331648 | bytes 27983884 | tf_op jit(solution)/shard_map/jit(_where)/select_n | solution.py:42
  350.9 13.9 %collective-permute-start.29 = (f32[16,1,32,256]{3,0,2,1:T(8,128)S(1)}, f32[16,1,32,256]{3,0,2,1:T(8,128)S(1)}, u32[]{:S(2)}, u32[]{:S(2)}) collective-permute-start(f32[16,1,32,256]{3,0,2,1:T(8,128)S(1)} %get-tuple-element.28), channel_id=1, source_target_pairs={{0,4},{4,8},{8,12},{12,16},{16,20},{20,24},{24,28},{1,5},{5,9},{9,... | collective-permute-start | bytes 1572872 | tf_op jit(solution)/shard_map/ppermute | solution.py:19
  377.7 22.7 %fusion.82 = f32[16,16,32,256]{3,0,2,1:T(8,128)} fusion(f32[16,16,32,256]{3,0,2,1:T(8,128)S(1)} %fusion.85, f32[16,16,32,256]{3,0,2,1:T(8,128)} %fusion.83, f32[16,1,32,256]{3,0,2,1:T(8,128)S(1)} %collective-permute-done.28, f32[16,1,32,256]{3,0,2,1:T(8,128)S(1)} %collective-permute-done.29, f32[16,18,1,256]{3,0,2,1:T(8,128)S(1)} %collective-permute-done.31, ...), kind=kLoop, calls=%fused_computation.159 | loop fusion | flops 50331648 | bytes 27983884 | tf_op jit(solution)/shard_map/jit(_where)/select_n | solution.py:42
  400.4 32.9 %copy.61 = f32[16,16,32,256]{0,3,2,1:T(8,128)} copy(f32[16,16,32,256]{3,0,2,1:T(8,128)} %fusion.82) | data formatting | bytes 16777216 | tf_op jit(solution)/shard_map/jit(_where)/select_n | solution.py:42
  436.0 39.7 %all-to-all-start = ((f32[32,1,128]{2,1,0:T(1,128)}), f32[32,1,128]{2,1,0:T(1,128)S(1)}, u32[]{:S(2)}, u32[]{:S(2)}) async-start(f32[32,1,128]{2,1,0:T(1,128)} %reshape.93), calls=%async_computation | async-start | bytes 32768 | tf_op jit(solution)/shard_map/all_to_all | solution.py:74
  475.7 11.6 %copy.66 = f32[16,16,32,256]{3,2,1,0:T(8,128)} copy(f32[16,16,32,256]{3,0,2,1:T(8,128)} %fusion.82) | data formatting | bytes 16777216
  489.2 40.6 %psum.7 = f32[16,16]{1,0:T(8,128)} all-reduce(f32[16,16]{1,0:T(8,128)S(1)} %fusion.109), channel_id=1, replica_groups=mesh['gx'=8,'gy'=4] {'gx','gy'}, use_global_device_ids=true, to_apply=%region_1.2 | all-reduce | flops 256 | bytes 2048 | tf_op jit(solution)/shard_map/psum | solution.py:81
  (108 shorter events, 112.0 us)
Async XLA Ops:
  13.3 12.8 %collective-permute-start = (f32[16,1,32,256]{3,0,2,1:T(8,128)S(1)}, f32[16,1,32,256]{3,0,2,1:T(8,128)S(1)}, u32[]{:S(2)}, u32[]{:S(2)}) collective-permute-start(f32[16,1,32,256]{3,0,2,1:T(8,128)S(1)} %get-tuple-element.42), channel_id=1, source_target_pairs={{4,0},{8,4},{12,8},{16,12},{20,16},{24,20},{28,24},{5,1},{9,5},{13... | collective-permute-start | bytes 1572872 | tf_op jit(solution)/shard_map/ppermute | solution.py:21
  28.0 9.0 %collective-permute-start.2 = (f32[16,18,1,256]{3,0,2,1:T(8,128)S(1)}, f32[16,18,1,256]{3,0,2,1:T(8,128)S(1)}, u32[]{:S(2)}, u32[]{:S(2)}) collective-permute-start(f32[16,18,1,256]{3,0,2,1:T(8,128)S(1)} %get-tuple-element.26), channel_id=1, source_target_pairs={{1,0},{2,1},{3,2},{5,4},{6,5},{7,6},{9,8},{10,9},{11,10},{13,12},{... | collective-permute-start | bytes 884744 | tf_op jit(solution)/shard_map/ppermute | solution.py:21
  29.3 9.2 %collective-permute-start.3 = (f32[16,18,1,256]{3,0,2,1:T(8,128)S(1)}, f32[16,18,1,256]{3,0,2,1:T(8,128)S(1)}, u32[]{:S(2)}, u32[]{:S(2)}) collective-permute-start(f32[16,18,1,256]{3,0,2,1:T(8,128)S(1)} %get-tuple-element.27), channel_id=1, source_target_pairs={{0,1},{1,2},{2,3},{4,5},{5,6},{6,7},{8,9},{9,10},{10,11},{12,13},{... | collective-permute-start | bytes 884744 | tf_op jit(solution)/shard_map/ppermute | solution.py:19
  65.0 9.1 %collective-permute-start.4 = (f32[16,1,32,256]{3,0,2,1:T(8,128)S(1)}, f32[16,1,32,256]{3,0,2,1:T(8,128)S(1)}, u32[]{:S(2)}, u32[]{:S(2)}) collective-permute-start(f32[16,1,32,256]{3,0,2,1:T(8,128)S(1)} %get-tuple-element.41), channel_id=1, source_target_pairs={{4,0},{8,4},{12,8},{16,12},{20,16},{24,20},{28,24},{5,1},{9,5},{13... | collective-permute-start | bytes 1572872 | tf_op jit(solution)/shard_map/ppermute | solution.py:21
  66.3 9.3 %collective-permute-start.5 = (f32[16,1,32,256]{3,0,2,1:T(8,128)S(1)}, f32[16,1,32,256]{3,0,2,1:T(8,128)S(1)}, u32[]{:S(2)}, u32[]{:S(2)}) collective-permute-start(f32[16,1,32,256]{3,0,2,1:T(8,128)S(1)} %get-tuple-element.40), channel_id=1, source_target_pairs={{0,4},{4,8},{8,12},{12,16},{16,20},{20,24},{24,28},{1,5},{5,9},{9,... | collective-permute-start | bytes 1572872 | tf_op jit(solution)/shard_map/ppermute | solution.py:19
  78.0 8.9 %collective-permute-start.7 = (f32[16,18,1,256]{3,0,2,1:T(8,128)S(1)}, f32[16,18,1,256]{3,0,2,1:T(8,128)S(1)}, u32[]{:S(2)}, u32[]{:S(2)}) collective-permute-start(f32[16,18,1,256]{3,0,2,1:T(8,128)S(1)} %get-tuple-element.25), channel_id=1, source_target_pairs={{0,1},{1,2},{2,3},{4,5},{5,6},{6,7},{8,9},{9,10},{10,11},{12,13},{... | collective-permute-start | bytes 884744 | tf_op jit(solution)/shard_map/ppermute | solution.py:19
  113.1 14.2 %collective-permute-start.8 = (f32[16,1,32,256]{3,0,2,1:T(8,128)S(1)}, f32[16,1,32,256]{3,0,2,1:T(8,128)S(1)}, u32[]{:S(2)}, u32[]{:S(2)}) collective-permute-start(f32[16,1,32,256]{3,0,2,1:T(8,128)S(1)} %get-tuple-element.39), channel_id=1, source_target_pairs={{4,0},{8,4},{12,8},{16,12},{20,16},{24,20},{28,24},{5,1},{9,5},{13... | collective-permute-start | bytes 1572872 | tf_op jit(solution)/shard_map/ppermute | solution.py:21
  114.4 14.4 %collective-permute-start.9 = (f32[16,1,32,256]{3,0,2,1:T(8,128)S(1)}, f32[16,1,32,256]{3,0,2,1:T(8,128)S(1)}, u32[]{:S(2)}, u32[]{:S(2)}) collective-permute-start(f32[16,1,32,256]{3,0,2,1:T(8,128)S(1)} %get-tuple-element.38), channel_id=1, source_target_pairs={{0,4},{4,8},{8,12},{12,16},{16,20},{20,24},{24,28},{1,5},{5,9},{9,... | collective-permute-start | bytes 1572872 | tf_op jit(solution)/shard_map/ppermute | solution.py:19
  131.2 8.9 %collective-permute-start.11 = (f32[16,18,1,256]{3,0,2,1:T(8,128)S(1)}, f32[16,18,1,256]{3,0,2,1:T(8,128)S(1)}, u32[]{:S(2)}, u32[]{:S(2)}) collective-permute-start(f32[16,18,1,256]{3,0,2,1:T(8,128)S(1)} %get-tuple-element.23), channel_id=1, source_target_pairs={{0,1},{1,2},{2,3},{4,5},{5,6},{6,7},{8,9},{9,10},{10,11},{12,13},{... | collective-permute-start | bytes 884744 | tf_op jit(solution)/shard_map/ppermute | solution.py:19
  166.1 11.4 %collective-permute-start.12 = (f32[16,1,32,256]{3,0,2,1:T(8,128)S(1)}, f32[16,1,32,256]{3,0,2,1:T(8,128)S(1)}, u32[]{:S(2)}, u32[]{:S(2)}) collective-permute-start(f32[16,1,32,256]{3,0,2,1:T(8,128)S(1)} %get-tuple-element.37), channel_id=1, source_target_pairs={{4,0},{8,4},{12,8},{16,12},{20,16},{24,20},{28,24},{5,1},{9,5},{13... | collective-permute-start | bytes 1572872 | tf_op jit(solution)/shard_map/ppermute | solution.py:21
  167.4 11.6 %collective-permute-start.13 = (f32[16,1,32,256]{3,0,2,1:T(8,128)S(1)}, f32[16,1,32,256]{3,0,2,1:T(8,128)S(1)}, u32[]{:S(2)}, u32[]{:S(2)}) collective-permute-start(f32[16,1,32,256]{3,0,2,1:T(8,128)S(1)} %get-tuple-element.36), channel_id=1, source_target_pairs={{0,4},{4,8},{8,12},{12,16},{16,20},{20,24},{24,28},{1,5},{5,9},{9,... | collective-permute-start | bytes 1572872 | tf_op jit(solution)/shard_map/ppermute | solution.py:19
  181.4 9.1 %collective-permute-start.15 = (f32[16,18,1,256]{3,0,2,1:T(8,128)S(1)}, f32[16,18,1,256]{3,0,2,1:T(8,128)S(1)}, u32[]{:S(2)}, u32[]{:S(2)}) collective-permute-start(f32[16,18,1,256]{3,0,2,1:T(8,128)S(1)} %get-tuple-element.21), channel_id=1, source_target_pairs={{0,1},{1,2},{2,3},{4,5},{5,6},{6,7},{8,9},{9,10},{10,11},{12,13},{... | collective-permute-start | bytes 884744 | tf_op jit(solution)/shard_map/ppermute | solution.py:19
  214.8 11.1 %collective-permute-start.16 = (f32[16,1,32,256]{3,0,2,1:T(8,128)S(1)}, f32[16,1,32,256]{3,0,2,1:T(8,128)S(1)}, u32[]{:S(2)}, u32[]{:S(2)}) collective-permute-start(f32[16,1,32,256]{3,0,2,1:T(8,128)S(1)} %get-tuple-element.35), channel_id=1, source_target_pairs={{4,0},{8,4},{12,8},{16,12},{20,16},{24,20},{28,24},{5,1},{9,5},{13... | collective-permute-start | bytes 1572872 | tf_op jit(solution)/shard_map/ppermute | solution.py:21
  216.1 11.3 %collective-permute-start.17 = (f32[16,1,32,256]{3,0,2,1:T(8,128)S(1)}, f32[16,1,32,256]{3,0,2,1:T(8,128)S(1)}, u32[]{:S(2)}, u32[]{:S(2)}) collective-permute-start(f32[16,1,32,256]{3,0,2,1:T(8,128)S(1)} %get-tuple-element.34), channel_id=1, source_target_pairs={{0,4},{4,8},{8,12},{12,16},{16,20},{20,24},{24,28},{1,5},{5,9},{9,... | collective-permute-start | bytes 1572872 | tf_op jit(solution)/shard_map/ppermute | solution.py:19
  228.7 9.1 %collective-permute-start.19 = (f32[16,18,1,256]{3,0,2,1:T(8,128)S(1)}, f32[16,18,1,256]{3,0,2,1:T(8,128)S(1)}, u32[]{:S(2)}, u32[]{:S(2)}) collective-permute-start(f32[16,18,1,256]{3,0,2,1:T(8,128)S(1)} %get-tuple-element.19), channel_id=1, source_target_pairs={{0,1},{1,2},{2,3},{4,5},{5,6},{6,7},{8,9},{9,10},{10,11},{12,13},{... | collective-permute-start | bytes 884744 | tf_op jit(solution)/shard_map/ppermute | solution.py:19
  252.2 11.1 %collective-permute-start.20 = (f32[16,1,32,256]{3,0,2,1:T(8,128)S(1)}, f32[16,1,32,256]{3,0,2,1:T(8,128)S(1)}, u32[]{:S(2)}, u32[]{:S(2)}) collective-permute-start(f32[16,1,32,256]{3,0,2,1:T(8,128)S(1)} %get-tuple-element.33), channel_id=1, source_target_pairs={{4,0},{8,4},{12,8},{16,12},{20,16},{24,20},{28,24},{5,1},{9,5},{13... | collective-permute-start | bytes 1572872 | tf_op jit(solution)/shard_map/ppermute | solution.py:21
  253.5 11.3 %collective-permute-start.21 = (f32[16,1,32,256]{3,0,2,1:T(8,128)S(1)}, f32[16,1,32,256]{3,0,2,1:T(8,128)S(1)}, u32[]{:S(2)}, u32[]{:S(2)}) collective-permute-start(f32[16,1,32,256]{3,0,2,1:T(8,128)S(1)} %get-tuple-element.32), channel_id=1, source_target_pairs={{0,4},{4,8},{8,12},{12,16},{16,20},{20,24},{24,28},{1,5},{5,9},{9,... | collective-permute-start | bytes 1572872 | tf_op jit(solution)/shard_map/ppermute | solution.py:19
  267.1 9.1 %collective-permute-start.23 = (f32[16,18,1,256]{3,0,2,1:T(8,128)S(1)}, f32[16,18,1,256]{3,0,2,1:T(8,128)S(1)}, u32[]{:S(2)}, u32[]{:S(2)}) collective-permute-start(f32[16,18,1,256]{3,0,2,1:T(8,128)S(1)} %get-tuple-element.17), channel_id=1, source_target_pairs={{0,1},{1,2},{2,3},{4,5},{5,6},{6,7},{8,9},{9,10},{10,11},{12,13},{... | collective-permute-start | bytes 884744 | tf_op jit(solution)/shard_map/ppermute | solution.py:19
  300.2 12.6 %collective-permute-start.24 = (f32[16,1,32,256]{3,0,2,1:T(8,128)S(1)}, f32[16,1,32,256]{3,0,2,1:T(8,128)S(1)}, u32[]{:S(2)}, u32[]{:S(2)}) collective-permute-start(f32[16,1,32,256]{3,0,2,1:T(8,128)S(1)} %get-tuple-element.31), channel_id=1, source_target_pairs={{4,0},{8,4},{12,8},{16,12},{20,16},{24,20},{28,24},{5,1},{9,5},{13... | collective-permute-start | bytes 1572872 | tf_op jit(solution)/shard_map/ppermute | solution.py:21
  301.5 12.8 %collective-permute-start.25 = (f32[16,1,32,256]{3,0,2,1:T(8,128)S(1)}, f32[16,1,32,256]{3,0,2,1:T(8,128)S(1)}, u32[]{:S(2)}, u32[]{:S(2)}) collective-permute-start(f32[16,1,32,256]{3,0,2,1:T(8,128)S(1)} %get-tuple-element.30), channel_id=1, source_target_pairs={{0,4},{4,8},{8,12},{12,16},{16,20},{20,24},{24,28},{1,5},{5,9},{9,... | collective-permute-start | bytes 1572872 | tf_op jit(solution)/shard_map/ppermute | solution.py:19
  316.7 8.9 %collective-permute-start.27 = (f32[16,18,1,256]{3,0,2,1:T(8,128)S(1)}, f32[16,18,1,256]{3,0,2,1:T(8,128)S(1)}, u32[]{:S(2)}, u32[]{:S(2)}) collective-permute-start(f32[16,18,1,256]{3,0,2,1:T(8,128)S(1)} %get-tuple-element.15), channel_id=1, source_target_pairs={{0,1},{1,2},{2,3},{4,5},{5,6},{6,7},{8,9},{9,10},{10,11},{12,13},{... | collective-permute-start | bytes 884744 | tf_op jit(solution)/shard_map/ppermute | solution.py:19
  349.6 15.5 %collective-permute-start.28 = (f32[16,1,32,256]{3,0,2,1:T(8,128)S(1)}, f32[16,1,32,256]{3,0,2,1:T(8,128)S(1)}, u32[]{:S(2)}, u32[]{:S(2)}) collective-permute-start(f32[16,1,32,256]{3,0,2,1:T(8,128)S(1)} %get-tuple-element.29), channel_id=1, source_target_pairs={{4,0},{8,4},{12,8},{16,12},{20,16},{24,20},{28,24},{5,1},{9,5},{13... | collective-permute-start | bytes 1572872 | tf_op jit(solution)/shard_map/ppermute | solution.py:21
  350.9 15.4 %collective-permute-start.29 = (f32[16,1,32,256]{3,0,2,1:T(8,128)S(1)}, f32[16,1,32,256]{3,0,2,1:T(8,128)S(1)}, u32[]{:S(2)}, u32[]{:S(2)}) collective-permute-start(f32[16,1,32,256]{3,0,2,1:T(8,128)S(1)} %get-tuple-element.28), channel_id=1, source_target_pairs={{0,4},{4,8},{8,12},{12,16},{16,20},{20,24},{24,28},{1,5},{5,9},{9,... | collective-permute-start | bytes 1572872 | tf_op jit(solution)/shard_map/ppermute | solution.py:19
  436.0 51.3 %all-to-all-start = ((f32[32,1,128]{2,1,0:T(1,128)}), f32[32,1,128]{2,1,0:T(1,128)S(1)}, u32[]{:S(2)}, u32[]{:S(2)}) async-start(f32[32,1,128]{2,1,0:T(1,128)} %reshape.93), calls=%async_computation | async-start | bytes 32768 | tf_op jit(solution)/shard_map/all_to_all | solution.py:74
  (17 other events, 299.8 us)
where the time goes:
time: 538 us; the launch traced here: 530 us
  other arithmetic  190 us (35%)
  starting transfers between devices  178 us (33%)
  local copies, waits for them, and re-layouts  79 us (15%)
  blocking collectives  40.6 us (8%)
  waiting for transfers between devices  39.9 us (7%)
    select_n x8, other arithmetic, relax(): return jnp.where(diffusion > 0.0, updated, 0.0)  180 us
    ppermute x16, starting transfers between devices, padded_2(): lax.ppermute(tail, axis, [(i, (i + 1) % count) for i in range(ends)])  117 us
    psum x1, blocking collectives, body(): lax.psum(jnp.dot(goal_block.T, goal_block, precision=lax.Precision.HIGHES...  40.6 us
    all_to_all x1, starting transfers between devices, body(): lax.all_to_all(outgoing, ('gx', 'gy'), split_axis=0, concat_axis=0, tiled...  39.7 us
    unnamed x22, local copies, waits for them, and re-layouts  33.4 us
    select_n x1, local copies, waits for them, and re-layouts, relax(): return jnp.where(diffusion > 0.0, updated, 0.0)  32.9 us
    ppermute x16, waiting for transfers between devices, padded_2(): lax.ppermute(tail, axis, [(i, (i + 1) % count) for i in range(ends)])  21.8 us
    ppermute x16, starting transfers between devices, padded_2(): lax.ppermute(head, axis, [((i + 1) % count, i) for i in range(ends)])  21.2 us
  transfers between devices with their start and end apart: 33, of which 22 were waited for; matrix products, arithmetic and copies ran while one was open for 5% of the time, Pallas kernels for 0%

commit v1 on v0

--- a/solution.py
+++ b/solution.py
@@ -2,6 +2,7 @@
 import jax.numpy as jnp
 from jax import lax
 from jax.sharding import PartitionSpec as P
+from jax.lax import all_gather
 
 STEPS = 2
 SWEEPS = 4
@@ -78,9 +79,9 @@
         received[..., :probe_count],
         precision=lax.Precision.HIGHEST,
     )
-    ritz_gram = lax.psum(
-        jnp.dot(goal_block.T, goal_block, precision=lax.Precision.HIGHEST), ("gx", "gy")
-    )
+    ritz_gram = all_gather(
+        jnp.dot(goal_block.T, goal_block, precision=lax.Precision.HIGHEST), axis_name=("gx", "gy")
+    ).sum(axis=0)
     return (state_field, goal_block, ritz_gram)
 
 

time: 538 us -> 568 us (1.056)
  blocking collectives: 40.6 us -> 70.7 us
    all_gather x0 -> x1, blocking collectives: none -> 70.7 us  [body(): all_gather(jnp.dot(goal_block.T, goal_block, precision=lax.Precision.HIGH...]
    psum x1 -> x0, blocking collectives: 40.6 us -> none  [body(): lax.psum(jnp.dot(goal_block.T, goal_block, precision=lax.Precision.HIGHES...]
where the time goes in v1:
time: 568 us; the launch traced here: 561 us
  other arithmetic  191 us (34%)
  starting transfers between devices  178 us (31%)
  local copies, waits for them, and re-layouts  79 us (14%)
  blocking collectives  70.7 us (12%)
  waiting for transfers between devices  39.9 us (7%)
    select_n x8, other arithmetic, relax(): return jnp.where(diffusion > 0.0, updated, 0.0)  180 us
    ppermute x16, starting transfers between devices, padded_2(): lax.ppermute(tail, axis, [(i, (i + 1) % count) for i in range(ends)])  117 us
    all_gather x1, blocking collectives, body(): all_gather(jnp.dot(goal_block.T, goal_block, precision=lax.Precision.HIGH...  70.7 us
    all_to_all x1, starting transfers between devices, body(): lax.all_to_all(outgoing, ('gx', 'gy'), split_axis=0, concat_axis=0, tiled...  39.7 us
    unnamed x22, local copies, waits for them, and re-layouts  33.4 us
    select_n x1, local copies, waits for them, and re-layouts, relax(): return jnp.where(diffusion > 0.0, updated, 0.0)  32.9 us
    ppermute x16, waiting for transfers between devices, padded_2(): lax.ppermute(tail, axis, [(i, (i + 1) % count) for i in range(ends)])  21.8 us
    ppermute x16, starting transfers between devices, padded_2(): lax.ppermute(head, axis, [((i + 1) % count, i) for i in range(ends)])  21.2 us
  transfers between devices with their start and end apart: 33, of which 22 were waited for; matrix products, arithmetic and copies ran while one was open for 5% of the time, Pallas kernels for 0%

profile of v1, /device:TPU:0, one launch (start us, length us, event | category | flops | bytes accessed | tf_op | source)
XLA Modules:
  0.0 560.8 jit_solution(7697988557552064644)
XLA Ops:
  0.7 10.1 %copy.60 = f32[16,16,32,256]{3,0,2,1:T(8,128)S(1)} copy(f32[16,16,32,256]{3,2,1,0:T(8,128)} %param.7) | data formatting | bytes 16777216 | tf_op args[0]
  16.0 10.0 %constant_dynamic-update-slice_fusion.1 = f32[16,18,32,256]{3,0,2,1:T(8,128)} fusion(f32[16,18,32,256]{3,0,2,1:T(8,128)} %constant_dynamic-update-slice_fusion.2, f32[16,16,32,256]{3,2,1,0:T(8,128)S(1)} %copy-done), kind=kLoop, calls=%fused_computation.202 | loop fusion | bytes 16777216
  29.3 4.9 collective-permute-start.3
  38.4 25.3 %fusion.81 = f32[16,16,32,256]{3,0,2,1:T(8,128)} fusion(f32[16,16,32,256]{3,0,2,1:T(8,128)} %copy-done.2, f32[16,18,32,256]{3,0,2,1:T(8,128)} %constant_dynamic-update-slice_fusion, f32[16,18,1,256]{3,0,2,1:T(8,128)S(1)} %collective-permute-done.3, f32[16,18,1,256]{3,0,2,1:T(8,128)S(1)} %collective-permute-done.2, ...), kind=kLoop, calls=%fused_computation.158 | loop fusion | flops 41943040 | bytes 29032460 | tf_op jit(solution)/shard_map/jit(_where)/select_n | solution.py:43
  66.3 7.8 %collective-permute-start.5 = (f32[16,1,32,256]{3,0,2,1:T(8,128)S(1)}, f32[16,1,32,256]{3,0,2,1:T(8,128)S(1)}, u32[]{:S(2)}, u32[]{:S(2)}) collective-permute-start(f32[16,1,32,256]{3,0,2,1:T(8,128)S(1)} %get-tuple-element.40), channel_id=1, source_target_pairs={{0,4},{4,8},{8,12},{12,16},{16,20},{20,24},{24,28},{1,5},{5,9},{9,... | collective-permute-start | bytes 1572872 | tf_op jit(solution)/shard_map/ppermute | solution.py:20
  78.0 4.9 collective-permute-start.7
  86.9 24.8 %fusion.87 = f32[16,16,32,256]{3,0,2,1:T(8,128)} fusion(f32[16,16,32,256]{3,0,2,1:T(8,128)} %fusion.81, f32[16,1,32,256]{3,0,2,1:T(8,128)S(1)} %collective-permute-done.4, f32[16,1,32,256]{3,0,2,1:T(8,128)S(1)} %collective-permute-done.5, f32[16,18,1,256]{3,0,2,1:T(8,128)S(1)} %collective-permute-done.7, f32[16,18,1,256]{3,0,2,1:T(8,128)S(1)} %collective-permute-done.6, ...), kind=kLoop, calls=%fused_computation.164 | loop fusion | flops 50331648 | bytes 27983884 | tf_op jit(solution)/shard_map/jit(_where)/select_n | solution.py:43
  114.4 12.9 %collective-permute-start.9 = (f32[16,1,32,256]{3,0,2,1:T(8,128)S(1)}, f32[16,1,32,256]{3,0,2,1:T(8,128)S(1)}, u32[]{:S(2)}, u32[]{:S(2)}) collective-permute-start(f32[16,1,32,256]{3,0,2,1:T(8,128)S(1)} %get-tuple-element.38), channel_id=1, source_target_pairs={{0,4},{4,8},{8,12},{12,16},{16,20},{20,24},{24,28},{1,5},{5,9},{9,... | collective-permute-start | bytes 1572872 | tf_op jit(solution)/shard_map/ppermute | solution.py:20
  140.1 24.8 %fusion.86 = f32[16,16,32,256]{3,0,2,1:T(8,128)} fusion(f32[16,16,32,256]{3,0,2,1:T(8,128)} %fusion.87, f32[16,1,32,256]{3,0,2,1:T(8,128)S(1)} %collective-permute-done.8, f32[16,1,32,256]{3,0,2,1:T(8,128)S(1)} %collective-permute-done.9, f32[16,18,1,256]{3,0,2,1:T(8,128)S(1)} %collective-permute-done.11, ...), kind=kLoop, calls=%fused_computation.163 | loop fusion | flops 50331648 | bytes 27983884 | tf_op jit(solution)/shard_map/jit(_where)/select_n | solution.py:43
  167.4 10.1 %collective-permute-start.13 = (f32[16,1,32,256]{3,0,2,1:T(8,128)S(1)}, f32[16,1,32,256]{3,0,2,1:T(8,128)S(1)}, u32[]{:S(2)}, u32[]{:S(2)}) collective-permute-start(f32[16,1,32,256]{3,0,2,1:T(8,128)S(1)} %get-tuple-element.36), channel_id=1, source_target_pairs={{0,4},{4,8},{8,12},{12,16},{16,20},{20,24},{24,28},{1,5},{5,9},{9,... | collective-permute-start | bytes 1572872 | tf_op jit(solution)/shard_map/ppermute | solution.py:20
  190.5 24.2 %fusion.85 = f32[16,16,32,256]{3,0,2,1:T(8,128)S(1)} fusion(f32[16,16,32,256]{3,0,2,1:T(8,128)} %fusion.86, f32[16,1,32,256]{3,0,2,1:T(8,128)S(1)} %collective-permute-done.12, f32[16,1,32,256]{3,0,2,1:T(8,128)S(1)} %collective-permute-done.13, f32[16,18,1,256]{3,0,2,1:T(8,128)S(1)} %collective-permute-done.15, ...), kind=kLoop, calls=%fused_computation.162 | loop fusion | flops 50331648 | bytes 27983884 | tf_op jit(solution)/shard_map/jit(_where)/select_n | solution.py:43
  216.1 9.8 %collective-permute-start.17 = (f32[16,1,32,256]{3,0,2,1:T(8,128)S(1)}, f32[16,1,32,256]{3,0,2,1:T(8,128)S(1)}, u32[]{:S(2)}, u32[]{:S(2)}) collective-permute-start(f32[16,1,32,256]{3,0,2,1:T(8,128)S(1)} %get-tuple-element.34), channel_id=1, source_target_pairs={{0,4},{4,8},{8,12},{12,16},{16,20},{20,24},{24,28},{1,5},{5,9},{9,... | collective-permute-start | bytes 1572872 | tf_op jit(solution)/shard_map/ppermute | solution.py:20
  228.7 5.1 collective-permute-start.19
  237.8 13.1 %fusion.80 = f32[16,16,32,256]{3,0,2,1:T(8,128)} fusion(f32[16,16,32,256]{3,0,2,1:T(8,128)S(1)} %fusion.85, f32[16,1,32,256]{3,0,2,1:T(8,128)S(1)} %collective-permute-done.16, f32[16,1,32,256]{3,0,2,1:T(8,128)S(1)} %collective-permute-done.17, f32[16,18,1,256]{3,0,2,1:T(8,128)S(1)} %collective-permute-done.19, ...), kind=kLoop, calls=%fused_computation.157 | loop fusion | flops 50331648 | bytes 19595276 | tf_op jit(solution)/shard_map/jit(_where)/select_n | solution.py:43
  253.5 9.8 %collective-permute-start.21 = (f32[16,1,32,256]{3,0,2,1:T(8,128)S(1)}, f32[16,1,32,256]{3,0,2,1:T(8,128)S(1)}, u32[]{:S(2)}, u32[]{:S(2)}) collective-permute-start(f32[16,1,32,256]{3,0,2,1:T(8,128)S(1)} %get-tuple-element.32), channel_id=1, source_target_pairs={{0,4},{4,8},{8,12},{12,16},{16,20},{20,24},{24,28},{1,5},{5,9},{9,... | collective-permute-start | bytes 1572872 | tf_op jit(solution)/shard_map/ppermute | solution.py:20
  276.2 22.7 %fusion.84 = f32[16,16,32,256]{3,0,2,1:T(8,128)} fusion(f32[16,16,32,256]{3,0,2,1:T(8,128)S(1)} %fusion.85, f32[16,16,32,256]{3,0,2,1:T(8,128)} %fusion.80, f32[16,1,32,256]{3,0,2,1:T(8,128)S(1)} %collective-permute-done.20, f32[16,1,32,256]{3,0,2,1:T(8,128)S(1)} %collective-permute-done.21, f32[16,18,1,256]{3,0,2,1:T(8,128)S(1)} %collective-permute-done.23, ...), kind=kLoop, calls=%fused_computation.161 | loop fusion | flops 50331648 | bytes 27983884 | tf_op jit(solution)/shard_map/jit(_where)/select_n | solution.py:43
  301.5 11.3 %collective-permute-start.25 = (f32[16,1,32,256]{3,0,2,1:T(8,128)S(1)}, f32[16,1,32,256]{3,0,2,1:T(8,128)S(1)}, u32[]{:S(2)}, u32[]{:S(2)}) collective-permute-start(f32[16,1,32,256]{3,0,2,1:T(8,128)S(1)} %get-tuple-element.30), channel_id=1, source_target_pairs={{0,4},{4,8},{8,12},{12,16},{16,20},{20,24},{24,28},{1,5},{5,9},{9,... | collective-permute-start | bytes 1572872 | tf_op jit(solution)/shard_map/ppermute | solution.py:20
  325.6 22.7 %fusion.83 = f32[16,16,32,256]{3,0,2,1:T(8,128)} fusion(f32[16,16,32,256]{3,0,2,1:T(8,128)S(1)} %fusion.85, f32[16,16,32,256]{3,0,2,1:T(8,128)} %fusion.84, f32[16,1,32,256]{3,0,2,1:T(8,128)S(1)} %collective-permute-done.24, f32[16,1,32,256]{3,0,2,1:T(8,128)S(1)} %collective-permute-done.25, f32[16,18,1,256]{3,0,2,1:T(8,128)S(1)} %collective-permute-done.27, ...), kind=kLoop, calls=%fused_computation.160 | loop fusion | flops 50331648 | bytes 27983884 | tf_op jit(solution)/shard_map/jit(_where)/select_n | solution.py:43
  350.9 13.9 %collective-permute-start.29 = (f32[16,1,32,256]{3,0,2,1:T(8,128)S(1)}, f32[16,1,32,256]{3,0,2,1:T(8,128)S(1)}, u32[]{:S(2)}, u32[]{:S(2)}) collective-permute-start(f32[16,1,32,256]{3,0,2,1:T(8,128)S(1)} %get-tuple-element.28), channel_id=1, source_target_pairs={{0,4},{4,8},{8,12},{12,16},{16,20},{20,24},{24,28},{1,5},{5,9},{9,... | collective-permute-start | bytes 1572872 | tf_op jit(solution)/shard_map/ppermute | solution.py:20
  377.7 22.7 %fusion.82 = f32[16,16,32,256]{3,0,2,1:T(8,128)} fusion(f32[16,16,32,256]{3,0,2,1:T(8,128)S(1)} %fusion.85, f32[16,16,32,256]{3,0,2,1:T(8,128)} %fusion.83, f32[16,1,32,256]{3,0,2,1:T(8,128)S(1)} %collective-permute-done.28, f32[16,1,32,256]{3,0,2,1:T(8,128)S(1)} %collective-permute-done.29, f32[16,18,1,256]{3,0,2,1:T(8,128)S(1)} %collective-permute-done.31, ...), kind=kLoop, calls=%fused_computation.159 | loop fusion | flops 50331648 | bytes 27983884 | tf_op jit(solution)/shard_map/jit(_where)/select_n | solution.py:43
  400.4 32.9 %copy.61 = f32[16,16,32,256]{0,3,2,1:T(8,128)} copy(f32[16,16,32,256]{3,0,2,1:T(8,128)} %fusion.82) | data formatting | bytes 16777216 | tf_op jit(solution)/shard_map/jit(_where)/select_n | solution.py:43
  436.0 39.7 %all-to-all-start = ((f32[32,1,128]{2,1,0:T(1,128)}), f32[32,1,128]{2,1,0:T(1,128)S(1)}, u32[]{:S(2)}, u32[]{:S(2)}) async-start(f32[32,1,128]{2,1,0:T(1,128)} %reshape.94), calls=%async_computation | async-start | bytes 32768 | tf_op jit(solution)/shard_map/all_to_all | solution.py:75
  475.7 11.6 %copy.66 = f32[16,16,32,256]{3,2,1,0:T(8,128)} copy(f32[16,16,32,256]{3,0,2,1:T(8,128)} %fusion.82) | data formatting | bytes 16777216
  489.2 70.7 %all-gather = f32[512,16]{1,0:T(8,128)S(1)} all-gather(f32[16,16]{1,0:T(8,128)S(1)} %fusion.109), channel_id=2, replica_groups=mesh['gx'=8,'gy'=4] {'gx','gy'}, dimensions={0}, use_global_device_ids=true | all-gather | bytes 33792 | tf_op jit(solution)/shard_map/all_gather | solution.py:82
  (109 shorter events, 112.6 us)
Async XLA Ops:
  13.3 12.8 %collective-permute-start = (f32[16,1,32,256]{3,0,2,1:T(8,128)S(1)}, f32[16,1,32,256]{3,0,2,1:T(8,128)S(1)}, u32[]{:S(2)}, u32[]{:S(2)}) collective-permute-start(f32[16,1,32,256]{3,0,2,1:T(8,128)S(1)} %get-tuple-element.42), channel_id=1, source_target_pairs={{4,0},{8,4},{12,8},{16,12},{20,16},{24,20},{28,24},{5,1},{9,5},{13... | collective-permute-start | bytes 1572872 | tf_op jit(solution)/shard_map/ppermute | solution.py:22
  28.0 9.0 %collective-permute-start.2 = (f32[16,18,1,256]{3,0,2,1:T(8,128)S(1)}, f32[16,18,1,256]{3,0,2,1:T(8,128)S(1)}, u32[]{:S(2)}, u32[]{:S(2)}) collective-permute-start(f32[16,18,1,256]{3,0,2,1:T(8,128)S(1)} %get-tuple-element.26), channel_id=1, source_target_pairs={{1,0},{2,1},{3,2},{5,4},{6,5},{7,6},{9,8},{10,9},{11,10},{13,12},{... | collective-permute-start | bytes 884744 | tf_op jit(solution)/shard_map/ppermute | solution.py:22
  29.3 9.2 %collective-permute-start.3 = (f32[16,18,1,256]{3,0,2,1:T(8,128)S(1)}, f32[16,18,1,256]{3,0,2,1:T(8,128)S(1)}, u32[]{:S(2)}, u32[]{:S(2)}) collective-permute-start(f32[16,18,1,256]{3,0,2,1:T(8,128)S(1)} %get-tuple-element.27), channel_id=1, source_target_pairs={{0,1},{1,2},{2,3},{4,5},{5,6},{6,7},{8,9},{9,10},{10,11},{12,13},{... | collective-permute-start | bytes 884744 | tf_op jit(solution)/shard_map/ppermute | solution.py:20
  65.0 9.1 %collective-permute-start.4 = (f32[16,1,32,256]{3,0,2,1:T(8,128)S(1)}, f32[16,1,32,256]{3,0,2,1:T(8,128)S(1)}, u32[]{:S(2)}, u32[]{:S(2)}) collective-permute-start(f32[16,1,32,256]{3,0,2,1:T(8,128)S(1)} %get-tuple-element.41), channel_id=1, source_target_pairs={{4,0},{8,4},{12,8},{16,12},{20,16},{24,20},{28,24},{5,1},{9,5},{13... | collective-permute-start | bytes 1572872 | tf_op jit(solution)/shard_map/ppermute | solution.py:22
  66.3 9.3 %collective-permute-start.5 = (f32[16,1,32,256]{3,0,2,1:T(8,128)S(1)}, f32[16,1,32,256]{3,0,2,1:T(8,128)S(1)}, u32[]{:S(2)}, u32[]{:S(2)}) collective-permute-start(f32[16,1,32,256]{3,0,2,1:T(8,128)S(1)} %get-tuple-element.40), channel_id=1, source_target_pairs={{0,4},{4,8},{8,12},{12,16},{16,20},{20,24},{24,28},{1,5},{5,9},{9,... | collective-permute-start | bytes 1572872 | tf_op jit(solution)/shard_map/ppermute | solution.py:20
  78.0 8.9 %collective-permute-start.7 = (f32[16,18,1,256]{3,0,2,1:T(8,128)S(1)}, f32[16,18,1,256]{3,0,2,1:T(8,128)S(1)}, u32[]{:S(2)}, u32[]{:S(2)}) collective-permute-start(f32[16,18,1,256]{3,0,2,1:T(8,128)S(1)} %get-tuple-element.25), channel_id=1, source_target_pairs={{0,1},{1,2},{2,3},{4,5},{5,6},{6,7},{8,9},{9,10},{10,11},{12,13},{... | collective-permute-start | bytes 884744 | tf_op jit(solution)/shard_map/ppermute | solution.py:20
  113.1 14.2 %collective-permute-start.8 = (f32[16,1,32,256]{3,0,2,1:T(8,128)S(1)}, f32[16,1,32,256]{3,0,2,1:T(8,128)S(1)}, u32[]{:S(2)}, u32[]{:S(2)}) collective-permute-start(f32[16,1,32,256]{3,0,2,1:T(8,128)S(1)} %get-tuple-element.39), channel_id=1, source_target_pairs={{4,0},{8,4},{12,8},{16,12},{20,16},{24,20},{28,24},{5,1},{9,5},{13... | collective-permute-start | bytes 1572872 | tf_op jit(solution)/shard_map/ppermute | solution.py:22
  114.4 14.4 %collective-permute-start.9 = (f32[16,1,32,256]{3,0,2,1:T(8,128)S(1)}, f32[16,1,32,256]{3,0,2,1:T(8,128)S(1)}, u32[]{:S(2)}, u32[]{:S(2)}) collective-permute-start(f32[16,1,32,256]{3,0,2,1:T(8,128)S(1)} %get-tuple-element.38), channel_id=1, source_target_pairs={{0,4},{4,8},{8,12},{12,16},{16,20},{20,24},{24,28},{1,5},{5,9},{9,... | collective-permute-start | bytes 1572872 | tf_op jit(solution)/shard_map/ppermute | solution.py:20
  131.2 8.9 %collective-permute-start.11 = (f32[16,18,1,256]{3,0,2,1:T(8,128)S(1)}, f32[16,18,1,256]{3,0,2,1:T(8,128)S(1)}, u32[]{:S(2)}, u32[]{:S(2)}) collective-permute-start(f32[16,18,1,256]{3,0,2,1:T(8,128)S(1)} %get-tuple-element.23), channel_id=1, source_target_pairs={{0,1},{1,2},{2,3},{4,5},{5,6},{6,7},{8,9},{9,10},{10,11},{12,13},{... | collective-permute-start | bytes 884744 | tf_op jit(solution)/shard_map/ppermute | solution.py:20
  166.1 11.4 %collective-permute-start.12 = (f32[16,1,32,256]{3,0,2,1:T(8,128)S(1)}, f32[16,1,32,256]{3,0,2,1:T(8,128)S(1)}, u32[]{:S(2)}, u32[]{:S(2)}) collective-permute-start(f32[16,1,32,256]{3,0,2,1:T(8,128)S(1)} %get-tuple-element.37), channel_id=1, source_target_pairs={{4,0},{8,4},{12,8},{16,12},{20,16},{24,20},{28,24},{5,1},{9,5},{13... | collective-permute-start | bytes 1572872 | tf_op jit(solution)/shard_map/ppermute | solution.py:22
  167.4 11.6 %collective-permute-start.13 = (f32[16,1,32,256]{3,0,2,1:T(8,128)S(1)}, f32[16,1,32,256]{3,0,2,1:T(8,128)S(1)}, u32[]{:S(2)}, u32[]{:S(2)}) collective-permute-start(f32[16,1,32,256]{3,0,2,1:T(8,128)S(1)} %get-tuple-element.36), channel_id=1, source_target_pairs={{0,4},{4,8},{8,12},{12,16},{16,20},{20,24},{24,28},{1,5},{5,9},{9,... | collective-permute-start | bytes 1572872 | tf_op jit(solution)/shard_map/ppermute | solution.py:20
  181.4 9.1 %collective-permute-start.15 = (f32[16,18,1,256]{3,0,2,1:T(8,128)S(1)}, f32[16,18,1,256]{3,0,2,1:T(8,128)S(1)}, u32[]{:S(2)}, u32[]{:S(2)}) collective-permute-start(f32[16,18,1,256]{3,0,2,1:T(8,128)S(1)} %get-tuple-element.21), channel_id=1, source_target_pairs={{0,1},{1,2},{2,3},{4,5},{5,6},{6,7},{8,9},{9,10},{10,11},{12,13},{... | collective-permute-start | bytes 884744 | tf_op jit(solution)/shard_map/ppermute | solution.py:20
  214.8 11.1 %collective-permute-start.16 = (f32[16,1,32,256]{3,0,2,1:T(8,128)S(1)}, f32[16,1,32,256]{3,0,2,1:T(8,128)S(1)}, u32[]{:S(2)}, u32[]{:S(2)}) collective-permute-start(f32[16,1,32,256]{3,0,2,1:T(8,128)S(1)} %get-tuple-element.35), channel_id=1, source_target_pairs={{4,0},{8,4},{12,8},{16,12},{20,16},{24,20},{28,24},{5,1},{9,5},{13... | collective-permute-start | bytes 1572872 | tf_op jit(solution)/shard_map/ppermute | solution.py:22
  216.1 11.3 %collective-permute-start.17 = (f32[16,1,32,256]{3,0,2,1:T(8,128)S(1)}, f32[16,1,32,256]{3,0,2,1:T(8,128)S(1)}, u32[]{:S(2)}, u32[]{:S(2)}) collective-permute-start(f32[16,1,32,256]{3,0,2,1:T(8,128)S(1)} %get-tuple-element.34), channel_id=1, source_target_pairs={{0,4},{4,8},{8,12},{12,16},{16,20},{20,24},{24,28},{1,5},{5,9},{9,... | collective-permute-start | bytes 1572872 | tf_op jit(solution)/shard_map/ppermute | solution.py:20
  228.7 9.1 %collective-permute-start.19 = (f32[16,18,1,256]{3,0,2,1:T(8,128)S(1)}, f32[16,18,1,256]{3,0,2,1:T(8,128)S(1)}, u32[]{:S(2)}, u32[]{:S(2)}) collective-permute-start(f32[16,18,1,256]{3,0,2,1:T(8,128)S(1)} %get-tuple-element.19), channel_id=1, source_target_pairs={{0,1},{1,2},{2,3},{4,5},{5,6},{6,7},{8,9},{9,10},{10,11},{12,13},{... | collective-permute-start | bytes 884744 | tf_op jit(solution)/shard_map/ppermute | solution.py:20
  252.2 11.1 %collective-permute-start.20 = (f32[16,1,32,256]{3,0,2,1:T(8,128)S(1)}, f32[16,1,32,256]{3,0,2,1:T(8,128)S(1)}, u32[]{:S(2)}, u32[]{:S(2)}) collective-permute-start(f32[16,1,32,256]{3,0,2,1:T(8,128)S(1)} %get-tuple-element.33), channel_id=1, source_target_pairs={{4,0},{8,4},{12,8},{16,12},{20,16},{24,20},{28,24},{5,1},{9,5},{13... | collective-permute-start | bytes 1572872 | tf_op jit(solution)/shard_map/ppermute | solution.py:22
  253.5 11.3 %collective-permute-start.21 = (f32[16,1,32,256]{3,0,2,1:T(8,128)S(1)}, f32[16,1,32,256]{3,0,2,1:T(8,128)S(1)}, u32[]{:S(2)}, u32[]{:S(2)}) collective-permute-start(f32[16,1,32,256]{3,0,2,1:T(8,128)S(1)} %get-tuple-element.32), channel_id=1, source_target_pairs={{0,4},{4,8},{8,12},{12,16},{16,20},{20,24},{24,28},{1,5},{5,9},{9,... | collective-permute-start | bytes 1572872 | tf_op jit(solution)/shard_map/ppermute | solution.py:20
  267.1 9.1 %collective-permute-start.23 = (f32[16,18,1,256]{3,0,2,1:T(8,128)S(1)}, f32[16,18,1,256]{3,0,2,1:T(8,128)S(1)}, u32[]{:S(2)}, u32[]{:S(2)}) collective-permute-start(f32[16,18,1,256]{3,0,2,1:T(8,128)S(1)} %get-tuple-element.17), channel_id=1, source_target_pairs={{0,1},{1,2},{2,3},{4,5},{5,6},{6,7},{8,9},{9,10},{10,11},{12,13},{... | collective-permute-start | bytes 884744 | tf_op jit(solution)/shard_map/ppermute | solution.py:20
  300.2 12.6 %collective-permute-start.24 = (f32[16,1,32,256]{3,0,2,1:T(8,128)S(1)}, f32[16,1,32,256]{3,0,2,1:T(8,128)S(1)}, u32[]{:S(2)}, u32[]{:S(2)}) collective-permute-start(f32[16,1,32,256]{3,0,2,1:T(8,128)S(1)} %get-tuple-element.31), channel_id=1, source_target_pairs={{4,0},{8,4},{12,8},{16,12},{20,16},{24,20},{28,24},{5,1},{9,5},{13... | collective-permute-start | bytes 1572872 | tf_op jit(solution)/shard_map/ppermute | solution.py:22
  301.5 12.8 %collective-permute-start.25 = (f32[16,1,32,256]{3,0,2,1:T(8,128)S(1)}, f32[16,1,32,256]{3,0,2,1:T(8,128)S(1)}, u32[]{:S(2)}, u32[]{:S(2)}) collective-permute-start(f32[16,1,32,256]{3,0,2,1:T(8,128)S(1)} %get-tuple-element.30), channel_id=1, source_target_pairs={{0,4},{4,8},{8,12},{12,16},{16,20},{20,24},{24,28},{1,5},{5,9},{9,... | collective-permute-start | bytes 1572872 | tf_op jit(solution)/shard_map/ppermute | solution.py:20
  316.7 8.9 %collective-permute-start.27 = (f32[16,18,1,256]{3,0,2,1:T(8,128)S(1)}, f32[16,18,1,256]{3,0,2,1:T(8,128)S(1)}, u32[]{:S(2)}, u32[]{:S(2)}) collective-permute-start(f32[16,18,1,256]{3,0,2,1:T(8,128)S(1)} %get-tuple-element.15), channel_id=1, source_target_pairs={{0,1},{1,2},{2,3},{4,5},{5,6},{6,7},{8,9},{9,10},{10,11},{12,13},{... | collective-permute-start | bytes 884744 | tf_op jit(solution)/shard_map/ppermute | solution.py:20
  349.6 15.5 %collective-permute-start.28 = (f32[16,1,32,256]{3,0,2,1:T(8,128)S(1)}, f32[16,1,32,256]{3,0,2,1:T(8,128)S(1)}, u32[]{:S(2)}, u32[]{:S(2)}) collective-permute-start(f32[16,1,32,256]{3,0,2,1:T(8,128)S(1)} %get-tuple-element.29), channel_id=1, source_target_pairs={{4,0},{8,4},{12,8},{16,12},{20,16},{24,20},{28,24},{5,1},{9,5},{13... | collective-permute-start | bytes 1572872 | tf_op jit(solution)/shard_map/ppermute | solution.py:22
  350.9 15.4 %collective-permute-start.29 = (f32[16,1,32,256]{3,0,2,1:T(8,128)S(1)}, f32[16,1,32,256]{3,0,2,1:T(8,128)S(1)}, u32[]{:S(2)}, u32[]{:S(2)}) collective-permute-start(f32[16,1,32,256]{3,0,2,1:T(8,128)S(1)} %get-tuple-element.28), channel_id=1, source_target_pairs={{0,4},{4,8},{8,12},{12,16},{16,20},{20,24},{24,28},{1,5},{5,9},{9,... | collective-permute-start | bytes 1572872 | tf_op jit(solution)/shard_map/ppermute | solution.py:20
  436.0 51.3 %all-to-all-start = ((f32[32,1,128]{2,1,0:T(1,128)}), f32[32,1,128]{2,1,0:T(1,128)S(1)}, u32[]{:S(2)}, u32[]{:S(2)}) async-start(f32[32,1,128]{2,1,0:T(1,128)} %reshape.94), calls=%async_computation | async-start | bytes 32768 | tf_op jit(solution)/shard_map/all_to_all | solution.py:75
  (17 other events, 330.5 us)
